TPU v7x, 32 devices: a whole 2x2x4 slice. The times are simulated.
32 devices in a mesh: dp: 8 (over z, x), mp: 4 (over y, core).
Axes of the slice: x: 2, y: 2, z: 4, core: 2. Of those that a mesh axis runs over, the one named last changes fastest.
Arguments:
- tokens: bfloat16 [16384, 1024], P('dp'), may hold values from -6 to 6
- segment_ids: int32 [8, 2048], P('dp'), may hold values from 0 to 127, never falling along the last dimension, each value on 1 to 512 neighbouring positions
- w_query: bfloat16 [1024, 1024], P(None, 'mp'), may hold values from -0.1875 to 0.1875
- w_key: bfloat16 [1024, 1024], P(None, 'mp'), may hold values from -0.1875 to 0.1875
- w_value: bfloat16 [1024, 1024], P(None, 'mp'), may hold values from -0.1875 to 0.1875
- w_gate: bfloat16 [1024, 1024], P(None, 'mp'), may hold values from -0.1875 to 0.1875
- w_out: bfloat16 [1024, 1024], P('mp'), may hold values from -0.25 to 0.25
- w_left: bfloat16 [1024, 2816], P(None, 'mp'), may hold values from -0.1875 to 0.1875
- w_right: bfloat16 [1024, 2816], P(None, 'mp'), may hold values from -0.1875 to 0.1875
- w_down: bfloat16 [2816, 1024], P('mp'), may hold values from -0.109375 to 0.109375
- cotangent: bfloat16 [16384, 1024], P('dp'), may hold values from -6 to 6
Outputs:
- output: bfloat16 [16384, 1024], P('dp')
- grad_tokens: bfloat16 [16384, 1024], P('dp')
- grad_w_query: float32 [1024, 1024], P('dp', 'mp')
- grad_w_key: float32 [1024, 1024], P('dp', 'mp')
- grad_w_value: float32 [1024, 1024], P('dp', 'mp')
- grad_w_gate: float32 [1024, 1024], P('dp', 'mp')
- grad_w_out: float32 [1024, 1024], P('mp', 'dp')
- grad_w_left: float32 [1024, 2816], P('dp', 'mp')
- grad_w_right: float32 [1024, 2816], P('dp', 'mp')
- grad_w_down: float32 [2816, 1024], P('mp', 'dp')
Inputs may be any that keep to these rules, and one draw needn't show every extreme that they name: `segment_ids`: in each row of 2048 positions the ids never fall; a document spans 1 to 512 positions, and one of them exactly that many.
All inputs are finite; a program needn't handle non-finite values.
Results may differ from a plain program's by a relative error of at most 0.02.
Values may be sent and summed in bfloat16 or wider, within the bound.
A program may use at most 192 MiB of HBM per device.

v0:
```python
import jax
import jax.numpy as jnp
from jax import lax
from jax.sharding import PartitionSpec as P

HD = 64
BLOCK = 64


def head_total(partial_value):
    return lax.psum(partial_value.astype(jnp.bfloat16), "mp").astype(jnp.float32)


def scatter_sum(grads):
    joined = jnp.concatenate([g.astype(jnp.bfloat16) for g in grads], axis=1)
    summed = lax.psum_scatter(joined, "dp", scatter_dimension=0, tiled=True).astype(jnp.float32)
    cuts = []
    at = 0
    for g in grads:
        cuts.append(summed[:, at : at + g.shape[1]])
        at += g.shape[1]
    return cuts


def rms_factor(values):
    return lax.rsqrt(jnp.mean(values * values, axis=-1, keepdims=True) + 1e-06)


def norm_back(grad, normed, factor):
    return factor * (grad - normed * jnp.mean(grad * normed, axis=-1, keepdims=True))


def block_scores(query_blocks, key_blocks, allowed):
    scores = jnp.einsum(
        "bqhd,bkhd->bhqk", query_blocks, key_blocks, preferred_element_type=jnp.float32
    ) * HD ** (-0.5)
    return jnp.where(allowed[:, None], scores, jnp.float32(-1e30))


def body(
    tokens, segment_ids, w_query, w_key, w_value, w_gate, w_out, w_left, w_right, w_down, cotangent
):
    rows_all = tokens.shape[0]
    width_c = w_query.shape[1]
    heads_here = width_c // HD
    blocks = rows_all // BLOCK
    source = tokens.astype(jnp.float32)
    recip_one = rms_factor(source)
    normed_one = source * recip_one
    normed_low = normed_one.astype(jnp.bfloat16)
    queries = jnp.dot(normed_low, w_query, preferred_element_type=jnp.float32).astype(jnp.bfloat16)
    keys_all = jnp.dot(normed_low, w_key, preferred_element_type=jnp.float32).astype(jnp.bfloat16)
    values_all = jnp.dot(normed_low, w_value, preferred_element_type=jnp.float32).astype(
        jnp.bfloat16
    )
    gate_pre = jnp.dot(normed_low, w_gate, preferred_element_type=jnp.float32).reshape(
        rows_all, heads_here, HD
    )
    query_blocks = queries.reshape(blocks, BLOCK, heads_here, HD)
    key_blocks = keys_all.reshape(blocks, BLOCK, heads_here, HD)
    value_blocks = values_all.reshape(blocks, BLOCK, heads_here, HD)
    seg_blocks = segment_ids.reshape(blocks, BLOCK)
    lower = jnp.arange(BLOCK)[:, None] >= jnp.arange(BLOCK)[None, :]
    allowed = (seg_blocks[:, :, None] == seg_blocks[:, None, :]) & lower[None]
    masked = block_scores(query_blocks, key_blocks, allowed)
    top = jnp.max(masked, axis=-1, keepdims=True)
    expd = jnp.exp(masked - top)
    total = jnp.sum(expd, axis=-1, keepdims=True)
    log_total = top + jnp.log(total)
    probs_low = (expd / total).astype(jnp.bfloat16)
    attended = jnp.einsum(
        "bhqk,bkhd->bqhd", probs_low, value_blocks, preferred_element_type=jnp.float32
    )
    attended = attended.reshape(rows_all, heads_here, HD)
    head_factor = rms_factor(attended)
    head_normed = attended * head_factor
    sigma = jax.nn.sigmoid(gate_pre)
    gated = (head_normed * sigma).reshape(rows_all, width_c).astype(jnp.bfloat16)
    attn_sum = head_total(jnp.dot(gated, w_out, preferred_element_type=jnp.float32))
    hidden = source + attn_sum
    recip_two = rms_factor(hidden)
    normed_two = hidden * recip_two
    normed_two_low = normed_two.astype(jnp.bfloat16)
    left = jnp.dot(normed_two_low, w_left, preferred_element_type=jnp.float32)
    right = jnp.dot(normed_two_low, w_right, preferred_element_type=jnp.float32)
    mixed = (left * right).astype(jnp.bfloat16)
    glu_sum = head_total(jnp.dot(mixed, w_down, preferred_element_type=jnp.float32))
    output = (hidden + glu_sum).astype(jnp.bfloat16)
    grad_down = jnp.einsum("tc,tf->cf", cotangent, mixed, preferred_element_type=jnp.float32)
    d_mixed = jnp.einsum("tc,fc->tf", cotangent, w_down, preferred_element_type=jnp.float32)
    d_left = (d_mixed * right).astype(jnp.bfloat16)
    d_right = (d_mixed * left).astype(jnp.bfloat16)
    grad_left = jnp.einsum("td,tf->df", normed_two_low, d_left, preferred_element_type=jnp.float32)
    grad_right = jnp.einsum(
        "td,tf->df", normed_two_low, d_right, preferred_element_type=jnp.float32
    )
    glu_grads = scatter_sum((grad_left, grad_right, grad_down))
    d_partial_two = jnp.einsum("tf,df->td", d_left, w_left, preferred_element_type=jnp.float32)
    d_partial_two = d_partial_two + jnp.einsum(
        "tf,df->td", d_right, w_right, preferred_element_type=jnp.float32
    )
    d_norm_two = head_total(d_partial_two)
    d_hidden = cotangent.astype(jnp.float32) + norm_back(d_norm_two, normed_two, recip_two)
    d_out_low = d_hidden.astype(jnp.bfloat16)
    grad_out = jnp.einsum("td,tc->dc", d_out_low, gated, preferred_element_type=jnp.float32)
    d_gated = jnp.einsum("td,cd->tc", d_out_low, w_out, preferred_element_type=jnp.float32)
    d_gated = d_gated.reshape(rows_all, heads_here, HD)
    d_head = d_gated * sigma
    d_gate = (
        (d_gated * head_normed * sigma * (1.0 - sigma))
        .reshape(rows_all, width_c)
        .astype(jnp.bfloat16)
    )
    d_attended = norm_back(d_head, head_normed, head_factor).astype(jnp.bfloat16)
    d_attended = d_attended.reshape(blocks, BLOCK, heads_here, HD)
    probs = jnp.exp(block_scores(query_blocks, key_blocks, allowed) - log_total)
    probs_back = probs.astype(jnp.bfloat16)
    d_probs = jnp.einsum(
        "bqhd,bkhd->bhqk", d_attended, value_blocks, preferred_element_type=jnp.float32
    )
    d_values = jnp.einsum(
        "bhqk,bqhd->bkhd", probs_back, d_attended, preferred_element_type=jnp.float32
    )
    delta_rows = jnp.sum(probs * d_probs, axis=-1, keepdims=True)
    d_scores = (probs * (d_probs - delta_rows)).astype(jnp.bfloat16)
    d_queries = jnp.einsum(
        "bhqk,bkhd->bqhd", d_scores, key_blocks, preferred_element_type=jnp.float32
    ) * HD ** (-0.5)
    d_keys = jnp.einsum(
        "bhqk,bqhd->bkhd", d_scores, query_blocks, preferred_element_type=jnp.float32
    ) * HD ** (-0.5)
    d_queries = d_queries.reshape(rows_all, width_c).astype(jnp.bfloat16)
    d_keys = d_keys.reshape(rows_all, width_c).astype(jnp.bfloat16)
    d_values = d_values.reshape(rows_all, width_c).astype(jnp.bfloat16)
    grad_query = jnp.einsum("td,tc->dc", normed_low, d_queries, preferred_element_type=jnp.float32)
    grad_key = jnp.einsum("td,tc->dc", normed_low, d_keys, preferred_element_type=jnp.float32)
    grad_value = jnp.einsum("td,tc->dc", normed_low, d_values, preferred_element_type=jnp.float32)
    grad_gate = jnp.einsum("td,tc->dc", normed_low, d_gate, preferred_element_type=jnp.float32)
    attn_grads = scatter_sum((grad_query, grad_key, grad_value, grad_gate, grad_out))
    d_partial_one = jnp.einsum("tc,dc->td", d_queries, w_query, preferred_element_type=jnp.float32)
    d_partial_one = d_partial_one + jnp.einsum(
        "tc,dc->td", d_keys, w_key, preferred_element_type=jnp.float32
    )
    d_partial_one = d_partial_one + jnp.einsum(
        "tc,dc->td", d_values, w_value, preferred_element_type=jnp.float32
    )
    d_partial_one = d_partial_one + jnp.einsum(
        "tc,dc->td", d_gate, w_gate, preferred_element_type=jnp.float32
    )
    d_norm_one = head_total(d_partial_one)
    d_source = d_hidden + norm_back(d_norm_one, normed_one, recip_one)
    grad_tokens = d_source.astype(jnp.bfloat16)
    return (
        output,
        grad_tokens,
        attn_grads[0],
        attn_grads[1],
        attn_grads[2],
        attn_grads[3],
        attn_grads[4].T,
        glu_grads[0],
        glu_grads[1],
        glu_grads[2].T,
    )


def solution(mesh):
    in_specs = (
        P("dp", None),
        P("dp", None),
        P(None, "mp"),
        P(None, "mp"),
        P(None, "mp"),
        P(None, "mp"),
        P("mp", None),
        P(None, "mp"),
        P(None, "mp"),
        P("mp", None),
        P("dp", None),
    )
    out_specs = (
        P("dp", None),
        P("dp", None),
        P("dp", "mp"),
        P("dp", "mp"),
        P("dp", "mp"),
        P("dp", "mp"),
        P("mp", "dp"),
        P("dp", "mp"),
        P("dp", "mp"),
        P("mp", "dp"),
    )
    return jax.shard_map(body, mesh=mesh, in_specs=in_specs, out_specs=out_specs, check_vma=False)
```

profile of v0, /device:TPU:0, one launch (start us, length us, event | category | flops | bytes accessed | tf_op | source)
XLA Modules:
  0.0 696.8 jit_solution(10704735771133625387)
XLA Ops:
  8.4 1.4 reduce.4
  9.8 3.2 fusion.10
  14.0 2.0 copy-done.20
  17.3 1.8 reshape.150
  19.1 3.0 copy.74
  22.1 5.3 convolution_convert_fusion.3
  27.4 4.4 reshape.149
  31.8 4.2 copy.78
  36.0 4.5 convolution_convert_fusion.4
  40.5 4.9 reshape.148
  46.4 2.8 fusion.48
  50.5 1.9 copy-done.30
  52.4 3.5 multiply_reduce_fusion.2
  57.3 6.6 copy.67
  64.0 3.6 reshape.151
  67.6 5.4 multiply_convert_fusion.7
  73.9 3.3 convolution_convert_fusion.1
  77.3 88.3 %all-reduce.5.cloned.1.call-done = bf16[2048,1024]{1,0:T(8,128)(2,1)} async-done(((bf16[2048,1024]{1,0:T(8,128)(2,1)}), bf16[2048,1024]{1,0:T(8,128)(2,1)}) %all-reduce.5.cloned.1.call-update) | async-done | bytes 4194320 | tf_op jit(solution)/shard_map/psum | solution.py:11
  165.6 5.0 multiply_reduce_fusion
  171.5 1.4 fusion.12
  173.0 3.2 fusion.50
  176.3 3.2 fusion.49
  179.5 5.5 multiply_convert_fusion
  185.0 6.0 fusion.51
  191.1 5.5 add_convert_fusion.1
  196.7 5.0 reshape.154
  201.6 1.6 log_add_fusion
  203.2 6.9 convolution_convert_fusion
  210.1 72.3 %all-reduce.7.cloned.1.call-done = bf16[2048,1024]{1,0:T(8,128)(2,1)} async-done(((bf16[2048,1024]{1,0:T(8,128)(2,1)}), bf16[2048,1024]{1,0:T(8,128)(2,1)}) %all-reduce.7.cloned.1.call-update) | async-done | bytes 4194320 | tf_op jit(solution)/shard_map/psum | solution.py:11
  282.4 6.6 fusion.3
  290.7 5.0 fusion.5
  295.8 4.2 multiply_reduce_fusion.3
  300.5 5.2 reshape.155
  305.8 6.6 fusion.14
  315.2 1.4 multiply_convert_fusion.5
  316.8 2.5 fusion.34
  319.4 2.6 fusion.33
  322.0 1.7 multiply_convert_fusion.6
  323.7 1.4 copy.83
  325.0 1.6 convert_element_type.173
  326.7 5.6 copy.77
  332.3 4.2 convert_element_type.166
  336.5 3.8 copy.81
  340.3 3.4 convert_element_type.169
  343.7 2.4 fusion.54
  346.2 4.7 fusion.53
  350.9 4.6 fusion.52
  355.5 9.9 %add_convert_fusion = bf16[2048,1024]{1,0:T(8,128)(2,1)} fusion(f32[2048,1024]{1,0:T(8,128)S(1)} %fusion.54, f32[2048,1024]{1,0:T(8,128)} %fusion.52, f32[2048,1024]{1,0:T(8,128)} %fusion.53, bf16[2048,256]{0,1:T(8,128)(2,1)S(1)} %copy-done.36, bf16[1024,256]{1,0:T(8,128)(2,1)S(1)} %copy-done.38), kind=kOutput, calls=%fused_computation.17 | convolution fusion | flops 1082130432 | bytes 30932992 | tf_op jit(solution)/shard_map/tc,dc->td/dot_general | solution.py:147
  365.4 4.4 fusion.45
  369.8 2.1 fusion.44
  371.9 2.1 fusion.43
  374.0 2.1 fusion.42
  376.1 2.1 fusion.39
  378.2 4.5 copy.95
  383.0 6.4 convolution_convert_fusion.5
  389.4 3.2 convolution_convert_fusion.6
  392.6 3.2 fusion.35
  395.7 2.4 pad_maximum_fusion
  398.2 6.6 copy.97
  404.8 113.8 %all-reduce.9.cloned.1.call-done = (bf16[2048,1024]{1,0:T(8,128)(2,1)}, bf16[2048,1024]{1,0:T(8,128)(2,1)}) async-done(((bf16[2048,1024]{1,0:T(8,128)(2,1)}, bf16[2048,1024]{1,0:T(8,128)(2,1)}), (bf16[2048,1024]{1,0:T(8,128)(2,1)}, bf16[2048,1024]{1,0:T(8,128)(2,1)})) %all-reduce.9.cloned.1.call-update) | async-done | bytes 8388624 | tf_op jit(solution)/shard_map/psum | solution.py:11
  518.6 4.5 fusion.9
  524.5 9.8 %fusion.8 = (bf16[2048,1024]{1,0:T(8,128)(2,1)}, bf16[2048,1024]{1,0:T(8,128)(2,1)}) fusion(f32[2048,1024]{1,0:T(8,128)} %copy-done.6, bf16[2048,1024]{1,0:T(8,128)(2,1)} %get-tuple-element.41, bf16[2048,1024]{1,0:T(8,128)(2,1)S(1)} %copy-done.5, f32[2048]{0:T(1024)S(1)} %broadcast_multiply_fusion.1, f32[2048]{0:T(1024)S(1)} %copy-done.51, ...), kind=kLoop, calls=%fused_computation.14 | loop fusion | flops 27262976 | bytes 33570816 | tf_op jit(solution)/shard_map/convert_element_type | solution.py:152
  534.3 58.6 %reduce-scatter.7.cloned.1.call-done = bf16[128,1280]{1,0:T(8,128)(2,1)} async-done(((bf16[1024,1280]{1,0:T(8,128)(2,1)}), bf16[128,1280]{1,0:T(8,128)(2,1)}) %reduce-scatter.7.cloned.1.call-update) | async-done | bytes 327696
  597.9 89.7 %reduce-scatter.9.cloned.1.call-done = bf16[128,2112]{1,0:T(8,128)(2,1)} async-done(((bf16[1024,2112]{1,0:T(8,128)(2,1)}), bf16[128,2112]{1,0:T(8,128)(2,1)}) %reduce-scatter.9.cloned.1.call-update) | async-done | bytes 540688
  (153 shorter events, 23.6 us)
Async XLA Ops:
  7.2 172.3 %copy-start = (bf16[704,1024]{1,0:T(8,128)(2,1)S(1)}, bf16[704,1024]{1,0:T(8,128)(2,1)}, u32[]{:S(2)}) copy-start(bf16[704,1024]{1,0:T(8,128)(2,1)} %param.20) | copy-start | bytes 4325380
  7.2 158.4 %all-reduce.5.cloned.1.call-start = ((), (), s32[]{:S(2)}) async-start(), calls=%async_computation.2 | async-start | bytes 8388608 | tf_op jit(solution)/shard_map/psum | solution.py:11
  9.8 3.5 copy-start.2
  13.2 0.8 copy-start.50
  13.2 2.8 copy-start.46
  14.0 2.0 copy-start.20
  22.1 24.3 %copy-start.17 = (bf16[32,64,4,64]{1,3,2,0:T(8,128)(2,1)}, bf16[32,64,4,64]{1,3,2,0:T(8,128)(2,1)S(1)}, u32[]{:S(2)}) copy-start(bf16[32,64,4,64]{1,3,2,0:T(8,128)(2,1)S(1)} %copy.74) | copy-start | bytes 3145732
  49.2 6.7 copy-start.7
  49.3 6.7 copy-start.42
  49.3 3.1 copy-start.30
  52.4 3.5 copy-start.49
  56.0 0.6 copy-start.43
  67.6 6.3 copy-start.39
  72.9 1.0 copy-start.22
  77.2 205.1 %all-reduce.7.cloned.1.call-start = ((), (), s32[]{:S(2)}) async-start(), calls=%async_computation.3 | async-start | bytes 8388608 | tf_op jit(solution)/shard_map/psum | solution.py:11
  165.6 5.0 copy-start.3
  165.6 5.9 copy-start.9
  171.5 1.5 copy-start.53
  173.0 3.3 copy-start.34
  173.0 3.3 copy-start.52
  176.3 3.3 copy-start.12
  185.0 6.0 copy-start.25
  185.0 6.0 copy-start.27
  185.0 6.0 copy-start.54
  196.6 321.9 %all-reduce.9.cloned.1.call-start = ((), (), s32[]{:S(2)}) async-start(), calls=%async_computation.6 | async-start | bytes 16777216 | tf_op jit(solution)/shard_map/psum | solution.py:11
  282.4 6.7 copy-start.4
  282.4 7.1 %copy-start.10 = (bf16[2048,1024]{1,0:T(8,128)(2,1)S(1)}, bf16[2048,1024]{1,0:T(8,128)(2,1)}, u32[]{:S(2)}) copy-start(bf16[2048,1024]{1,0:T(8,128)(2,1)} %all-reduce.5.cloned.1.call-done) | copy-start | bytes 12582916
  282.4 8.3 %copy-start.13 = (bf16[2048,1024]{1,0:T(8,128)(2,1)S(1)}, bf16[2048,1024]{1,0:T(8,128)(2,1)}, u32[]{:S(2)}) copy-start(bf16[2048,1024]{1,0:T(8,128)(2,1)} %param.21) | copy-start | bytes 12582916
  290.7 5.1 copy-start.15
  290.7 5.1 copy-start.29
  290.7 5.1 copy-start.40
  290.7 5.1 copy-start.45
  295.8 4.6 copy-start.6
  300.3 5.4 copy-start.44
  305.7 6.6 copy-start.8
  305.8 6.6 copy-start.41
  312.3 1.6 copy-start.31
  315.2 1.6 copy-start.19
  316.8 2.5 copy-start.18
  319.4 2.6 copy-start.16
  319.4 2.6 copy-start.28
  326.7 9.8 %copy-start.32 = (bf16[32,64,4,64]{3,1,2,0:T(8,128)(2,1)S(1)}, bf16[32,64,4,64]{3,1,2,0:T(8,128)(2,1)}, u32[]{:S(2)}) copy-start(bf16[32,64,4,64]{3,1,2,0:T(8,128)(2,1)} %fusion.34) | copy-start | bytes 3145732
  343.7 2.4 copy-start.47
  346.2 4.7 copy-start.33
  346.2 4.7 copy-start.48
  350.8 4.6 copy-start.36
  350.8 4.6 copy-start.38
  365.4 227.5 %reduce-scatter.7.cloned.1.call-start = ((), (), s32[]{:S(2)}) async-start(), calls=%async_computation.4 | async-start | bytes 2949120
  365.4 4.4 copy-start.21
  369.8 6.3 slice-start
  371.9 2.1 copy-start.37
  371.9 4.2 slice-start.1
  374.0 2.1 copy-start.23
  382.7 304.9 %reduce-scatter.9.cloned.1.call-start = ((), (), s32[]{:S(2)}) async-start(), calls=%async_computation.5 | async-start | bytes 5013504
  382.9 6.4 copy-start.26
  383.0 6.4 copy-start.35
  389.4 3.2 copy-start.14
  389.4 3.2 copy-start.24
  404.7 113.8 %copy-start.51 = (f32[2048]{0:T(1024)S(1)}, f32[2048]{0:T(1024)}, u32[]{:S(2)}) copy-start(f32[2048]{0:T(1024)} %copy-done.50) | copy-start | bytes 24580
  518.6 4.7 copy-start.5
  518.6 5.9 copy-start.11
  592.9 97.2 %copy-start.1 = (bf16[704,1024]{1,0:T(8,128)(2,1)S(1)}, bf16[704,1024]{1,0:T(8,128)(2,1)}, u32[]{:S(2)}) copy-start(bf16[704,1024]{1,0:T(8,128)(2,1)} %param.20) | copy-start | bytes 4325380
Sparse Core Ops, SparseCore 0:
  77.4 88.1 all-reduce.4
  196.7 85.6 all-reduce.6
  365.5 153.0 all-reduce.8
  521.9 70.8 reduce-scatter.6
  596.3 91.2 reduce-scatter.8
where the time goes:
time: 705 us; the launch traced here: 697 us
  waiting for transfers between devices  423 us (60%)
  matrix products  115 us (16%)
  local copies, waits for them, and re-layouts  89.2 us (13%)
  other arithmetic  54.5 us (8%)
  between operations  14.7 us (2%)
    psum x3, waiting for transfers between devices, head_total(): lax.psum(partial_value.astype(jnp.bfloat16), 'mp').astype(jnp.float32)  274 us
    unnamed x7, waiting for transfers between devices  148 us
    unnamed x123, local copies, waits for them, and re-layouts  27.9 us
  transfers between devices with their start and end apart: 5, of which 5 were waited for; matrix products, arithmetic and copies ran while one was open for 10% of the time, Pallas kernels for 0%

commit v1 on v0

--- a/solution.py
+++ b/solution.py
@@ -5,10 +5,11 @@
 
 HD = 64
 BLOCK = 64
+task_treat = lambda message, device_axis: lax.all_gather(message, axis_name=device_axis).sum(axis=0)
 
 
 def head_total(partial_value):
-    return lax.psum(partial_value.astype(jnp.bfloat16), "mp").astype(jnp.float32)
+    return task_treat(partial_value.astype(jnp.bfloat16), "mp").astype(jnp.float32)
 
 
 def scatter_sum(grads):

time: 705 us -> 754 us (1.070)
  other arithmetic: 54.5 us -> 101 us
  matrix products: 115 us -> 123 us
    all_gather x0 -> x4, waiting for transfers between devices: none -> 372 us  [lax.all_gather(message, axis_name=device_axis).sum(axis=0)]
    psum x3 -> x0, waiting for transfers between devices: 274 us -> none  [head_total(): lax.psum(partial_value.astype(jnp.bfloat16), 'mp').astype(jnp.float32)]
    unnamed x7 -> x8, waiting for transfers between devices: 148 us -> 46.6 us
    reduce_sum x0 -> x4, other arithmetic: none -> 49.4 us  [lax.all_gather(message, axis_name=device_axis).sum(axis=0)]
  transfers between devices with their start and end apart: 5 -> 6, of which waited for: 5 -> 5; matrix products, arithmetic and copies ran while one was open for 10% -> 24% of each run, Pallas kernels for 0% -> 0%
where the time goes in v1:
time: 754 us; the launch traced here: 746 us
  waiting for transfers between devices  418 us (55%)
  matrix products  123 us (16%)
  other arithmetic  101 us (13%)
  local copies, waits for them, and re-layouts  88.3 us (12%)
  between operations  15 us (2%)
    all_gather x4, waiting for transfers between devices, lax.all_gather(message, axis_name=device_axis).sum(axis=0)  372 us
    reduce_sum x4, other arithmetic, lax.all_gather(message, axis_name=device_axis).sum(axis=0)  49.4 us
    unnamed x8, waiting for transfers between devices  46.6 us
    unnamed x123, local copies, waits for them, and re-layouts  29.1 us
  transfers between devices with their start and end apart: 6, of which 5 were waited for; matrix products, arithmetic and copies ran while one was open for 24% of the time, Pallas kernels for 0%

profile of v1, /device:TPU:0, one launch (start us, length us, event | category | flops | bytes accessed | tf_op | source)
XLA Modules:
  0.0 746.2 jit_solution(3804545798659255427)
XLA Ops:
  9.8 3.2 fusion.10
  14.0 2.0 copy-done.21
  16.0 2.2 convolution_convert_fusion.2
  18.3 3.3 reshape.150
  21.6 2.4 copy.74
  24.0 3.6 convolution_convert_fusion.3
  29.3 3.0 copy.78
  32.3 5.3 convolution_convert_fusion.4
  37.6 4.6 reshape.148
  43.3 2.8 fusion.48
  47.4 1.9 copy-done.29
  49.3 3.5 multiply_reduce_fusion.2
  54.2 6.6 copy.67
  60.8 3.6 reshape.151
  64.4 6.0 multiply_convert_fusion.7
  71.5 3.3 convolution_convert_fusion.1
  74.8 108.7 %all-gather.9.cloned.1.call-done = bf16[8192,1024]{1,0:T(8,128)(2,1)} async-done(((bf16[2048,1024]{1,0:T(8,128)(2,1)}), bf16[8192,1024]{1,0:T(8,128)(2,1)}) %all-gather.9.cloned.1.call-update) | async-done | bytes 16777232 | tf_op jit(solution)/shard_map/all_gather | solution.py:8
  183.6 12.3 %reduce_sum.123 = bf16[2048,1024]{1,0:T(8,128)(2,1)} reduce(bf16[4,2048,1024]{2,1,0:T(8,128)(2,1)} %bitcast.116, bf16[]{:T(256)} %constant.28.clone.1), dimensions={0}, to_apply=%region_4.5 | reduce | flops 6291456 | bytes 20971522 | tf_op jit(solution)/shard_map/reduce_sum | solution.py:8
  195.9 5.0 multiply_reduce_fusion
  203.2 3.2 fusion.50
  206.4 3.2 fusion.49
  209.6 5.5 multiply_convert_fusion
  216.7 5.0 convolution_convert_fusion
  222.2 5.5 fusion.51
  227.8 5.3 add_convert_fusion.1
  233.2 7.5 %convolution_convert_fusion.5 = bf16[1024,704]{0,1:T(8,128)(2,1)S(1)} fusion(bf16[2048,704]{0,1:T(8,128)(2,1)} %get-tuple-element.44, bf16[2048,1024]{1,0:T(8,128)(2,1)} %copy-done.34), kind=kOutput, calls=%fused_computation.66 | convolution fusion | flops 2953510912 | bytes 8519680 | tf_op jit(solution)/shard_map/td,tf->df/dot_general | solution.py:95
  241.3 3.2 convolution_convert_fusion.6
  244.5 3.2 fusion.35
  247.7 2.4 pad_maximum_fusion
  250.1 6.4 copy.97
  256.7 5.0 reshape.154
  261.8 66.0 %all-gather.11.cloned.1.call-done = bf16[8192,1024]{1,0:T(8,128)(2,1)} async-done(((bf16[2048,1024]{1,0:T(8,128)(2,1)}), bf16[8192,1024]{1,0:T(8,128)(2,1)}) %all-gather.11.cloned.1.call-update) | async-done | bytes 16777232 | tf_op jit(solution)/shard_map/all_gather | solution.py:8
  327.8 12.8 %reduce_sum.125 = bf16[2048,1024]{1,0:T(8,128)(2,1)} reduce(bf16[4,2048,1024]{2,1,0:T(8,128)(2,1)} %bitcast.113, bf16[]{:T(256)} %constant.28.clone.1), dimensions={0}, to_apply=%region_6.7 | reduce | flops 6291456 | bytes 20971522 | tf_op jit(solution)/shard_map/reduce_sum | solution.py:8
  340.6 94.7 %all-gather.13.cloned.1.call-done = bf16[8192,1024]{1,0:T(8,128)(2,1)} async-done(((bf16[2048,1024]{1,0:T(8,128)(2,1)}), bf16[8192,1024]{1,0:T(8,128)(2,1)}) %all-gather.13.cloned.1.call-update) | async-done | bytes 16777232 | tf_op jit(solution)/shard_map/all_gather | solution.py:8
  435.3 12.1 %reduce_sum.126 = bf16[2048,1024]{1,0:T(8,128)(2,1)} reduce(bf16[4,2048,1024]{2,1,0:T(8,128)(2,1)} %bitcast.115, bf16[]{:T(256)} %constant.28.clone.1), dimensions={0}, to_apply=%region_7.8 | reduce | flops 6291456 | bytes 20971522 | tf_op jit(solution)/shard_map/reduce_sum | solution.py:8
  447.4 6.8 fusion.3
  455.8 7.2 fusion.5
  463.1 7.0 multiply_reduce_fusion.3
  472.0 3.2 reshape.155
  475.2 6.6 fusion.14
  483.1 2.8 copy.83
  485.9 3.4 convert_element_type.181
  489.3 4.7 multiply_reduce_fusion.1
  495.6 2.6 fusion.33
  498.2 5.3 copy.77
  503.5 4.6 convert_element_type.174
  508.1 4.4 fusion.34
  512.5 4.5 copy.81
  517.0 2.4 convert_element_type.177
  519.4 4.8 fusion.45
  524.2 2.1 fusion.44
  526.3 2.1 fusion.43
  528.4 2.1 fusion.42
  530.5 2.1 fusion.39
  532.6 4.5 copy.95
  537.4 2.4 fusion.54
  539.8 4.6 fusion.53
  544.4 4.7 fusion.52
  549.1 10.0 %add_convert_fusion = bf16[2048,1024]{1,0:T(8,128)(2,1)} fusion(f32[2048,1024]{1,0:T(8,128)S(1)} %fusion.54, f32[2048,1024]{1,0:T(8,128)} %fusion.52, f32[2048,1024]{1,0:T(8,128)} %fusion.53, bf16[2048,256]{0,1:T(8,128)(2,1)S(1)} %copy-done.36, bf16[1024,256]{1,0:T(8,128)(2,1)S(1)} %copy-done.37), kind=kOutput, calls=%fused_computation.17 | convolution fusion | flops 1082130432 | bytes 30932992 | tf_op jit(solution)/shard_map/tc,dc->td/dot_general | solution.py:148
  561.6 46.5 %reduce-scatter.7.cloned.1.call-done = bf16[128,1280]{1,0:T(8,128)(2,1)} async-done(((bf16[1024,1280]{1,0:T(8,128)(2,1)}), bf16[128,1280]{1,0:T(8,128)(2,1)}) %reduce-scatter.7.cloned.1.call-update) | async-done | bytes 327696
  613.0 102.1 %all-gather.15.cloned.1.call-done = bf16[8192,1024]{1,0:T(8,128)(2,1)} async-done(((bf16[2048,1024]{1,0:T(8,128)(2,1)}), bf16[8192,1024]{1,0:T(8,128)(2,1)}) %all-gather.15.cloned.1.call-update) | async-done | bytes 16777232 | tf_op jit(solution)/shard_map/all_gather | solution.py:8
  715.1 12.1 %reduce_sum.130 = bf16[2048,1024]{1,0:T(8,128)(2,1)} reduce(bf16[4,2048,1024]{2,1,0:T(8,128)(2,1)} %bitcast.114, bf16[]{:T(256)} %constant.28.clone.1), dimensions={0}, to_apply=%region_11.12 | reduce | flops 6291456 | bytes 20971522 | tf_op jit(solution)/shard_map/reduce_sum | solution.py:8
  727.3 4.5 fusion.9
  733.2 6.0 fusion.8
  (160 shorter events, 30.8 us)
Async XLA Ops:
  7.2 202.4 %copy-start = (bf16[704,1024]{1,0:T(8,128)(2,1)S(1)}, bf16[704,1024]{1,0:T(8,128)(2,1)}, u32[]{:S(2)}) copy-start(bf16[704,1024]{1,0:T(8,128)(2,1)} %param.20) | copy-start | bytes 4325380
  7.2 176.4 %all-gather.9.cloned.1.call-start = ((), (), s32[]{:S(2)}) async-start(), calls=%async_computation.2 | async-start | bytes 20971520 | tf_op jit(solution)/shard_map/all_gather | solution.py:8
  9.8 3.5 copy-start.2
  13.2 0.8 copy-start.50
  13.2 2.8 copy-start.45
  14.0 2.0 copy-start.21
  32.3 11.0 %copy-start.19 = (bf16[32,64,4,64]{1,3,2,0:T(8,128)(2,1)}, bf16[32,64,4,64]{1,3,2,0:T(8,128)(2,1)S(1)}, u32[]{:S(2)}) copy-start(bf16[32,64,4,64]{1,3,2,0:T(8,128)(2,1)S(1)} %copy.78) | copy-start | bytes 3145732
  46.1 6.6 copy-start.7
  46.1 6.6 copy-start.40
  46.1 3.1 copy-start.29
  49.3 3.5 copy-start.48
  52.8 0.6 copy-start.42
  64.4 6.1 copy-start.16
  64.4 7.0 copy-start.38
  70.5 1.0 copy-start.23
  74.8 253.0 %all-gather.11.cloned.1.call-start = ((), (), s32[]{:S(2)}) async-start(), calls=%async_computation.3 | async-start | bytes 20971520 | tf_op jit(solution)/shard_map/all_gather | solution.py:8
  195.9 5.0 copy-start.3
  195.9 5.9 copy-start.10
  201.8 1.4 copy-start.53
  203.2 3.2 copy-start.34
  203.2 3.2 copy-start.52
  206.4 3.2 copy-start.14
  215.1 1.6 copy-start.25
  221.7 213.6 %all-gather.13.cloned.1.call-start = ((), (), s32[]{:S(2)}) async-start(), calls=%async_computation.4 | async-start | bytes 20971520 | tf_op jit(solution)/shard_map/all_gather | solution.py:8
  222.2 5.6 copy-start.28
  222.2 5.6 copy-start.54
  233.1 326.0 %reduce-scatter.9.cloned.1.call-start = ((), (), s32[]{:S(2)}) async-start(), calls=%async_computation.7 | async-start | bytes 5013504
  233.2 7.5 %copy-start.27 = (bf16[2048,704]{0,1:T(8,128)(2,1)S(1)}, bf16[2048,704]{0,1:T(8,128)(2,1)}, u32[]{:S(2)}) copy-start(bf16[2048,704]{0,1:T(8,128)(2,1)} %get-tuple-element.46) | copy-start | bytes 8650756
  233.2 8.1 %copy-start.35 = (bf16[2048,1024]{1,0:T(8,128)(2,1)S(1)}, bf16[2048,1024]{1,0:T(8,128)(2,1)}, u32[]{:S(2)}) copy-start(bf16[2048,1024]{1,0:T(8,128)(2,1)} %copy-done.34) | copy-start | bytes 12582916
  241.3 3.2 copy-start.15
  241.3 3.2 copy-start.26
  256.5 5.3 copy-start.41
  256.5 5.3 copy-start.49
  256.5 351.5 %reduce-scatter.7.cloned.1.call-start = ((), (), s32[]{:S(2)}) async-start(), calls=%async_computation.6 | async-start | bytes 2949120
  447.4 6.8 copy-start.4
  447.4 7.2 copy-start.11
  447.4 8.4 %copy-start.13 = (bf16[2048,1024]{1,0:T(8,128)(2,1)S(1)}, bf16[2048,1024]{1,0:T(8,128)(2,1)}, u32[]{:S(2)}) copy-start(bf16[2048,1024]{1,0:T(8,128)(2,1)} %reduce_sum.126) | copy-start | bytes 12582916
  455.8 7.2 copy-start.39
  455.8 7.2 copy-start.44
  463.0 7.0 copy-start.6
  463.1 7.0 copy-start.17
  463.1 7.0 copy-start.18
  471.8 3.4 copy-start.43
  475.2 6.7 copy-start.8
  489.3 37.0 %copy-start.30 = (bf16[2048,256]{0,1:T(8,128)(2,1)}, bf16[2048,256]{0,1:T(8,128)(2,1)S(1)}, u32[]{:S(2)}) copy-start(bf16[2048,256]{0,1:T(8,128)(2,1)S(1)} %convert_element_type.181) | copy-start | bytes 3145732
  489.3 4.7 copy-start.9
  494.0 1.6 copy-start.20
  519.4 4.8 copy-start.22
  519.4 4.8 copy-start.33
  524.2 6.3 slice-start
  526.3 2.1 copy-start.36
  526.3 4.2 slice-start.1
  528.4 2.1 copy-start.24
  532.6 4.7 copy-start.31
  537.1 178.0 %all-gather.15.cloned.1.call-start = ((), (), s32[]{:S(2)}) async-start(), calls=%async_computation.5 | async-start | bytes 20971520 | tf_op jit(solution)/shard_map/all_gather | solution.py:8
  537.3 2.4 copy-start.46
  539.8 4.6 copy-start.32
  539.8 4.6 copy-start.47
  544.4 4.7 copy-start.37
  715.1 12.1 %copy-start.51 = (f32[2048]{0:T(1024)S(1)}, f32[2048]{0:T(1024)}, u32[]{:S(2)}) copy-start(f32[2048]{0:T(1024)} %copy-done.50) | copy-start | bytes 24580
  727.3 4.7 copy-start.5
  727.3 5.9 copy-start.12
  733.2 6.0 copy-start.1
Sparse Core Ops, SparseCore 0:
  74.9 108.6 all-gather.8
  221.9 105.8 all-gather.10
  329.4 105.8 all-gather.12
  438.8 92.0 reduce-scatter.8
  537.2 70.7 reduce-scatter.6
  610.0 105.0 all-gather.14
